TPU v7x, 256 devices: a whole 4x4x8 slice. The times are simulated.
256 devices in a mesh: expert: 32 (over z_hi, y, core), dp: 8 (over z_lo, x).
Axes of the slice: x: 4, y: 4, z: 8 (z_hi: 4, z_lo: 2; z = z_hi * 2 + z_lo), core: 2. Of those that a mesh axis runs over, the one named last changes fastest.
Arguments:
- tokens: bfloat16 [32768, 4096], P(('expert', 'dp')), may hold values from -6 to 6
- route: int32 [32768, 2], P(('expert', 'dp')), may hold values from 0 to 63, all different within a row; in each aligned block of 128 rows (0 to 127, 128 to 255, ...) at most 12 rows name the same one
- gate_output_gradient: bfloat16 [32768, 2, 1536], P(('expert', 'dp')), may hold values from -0.4375 to 0.4375
- frozen_gate_weight: bfloat16 [64, 4096, 1536], P('expert', 'dp'), may hold values from -0.09375 to 0.09375
- adapter_first: bfloat16 [64, 4096, 16], P('expert'), may hold values from -0.09375 to 0.09375
- adapter_second: bfloat16 [64, 16, 1536], P('expert'), may hold values from -0.15625 to 0.15625
Outputs:
- grad_a: float32 [64, 4096, 16], P('expert')
- grad_b: float32 [64, 16, 1536], P('expert')
Inputs may be any that keep to these rules, and one draw needn't show every extreme that they name: `route`: each row names 2 different experts. Within each device's aligned block of 128 rows no expert is named more than 12 times.
All inputs are finite; a program needn't handle non-finite values.
Results may differ from a plain program's by a relative error of at most 0.0043.
Values may be sent and summed in bfloat16 or wider, within the bound.
No kernel may reach another device: no remote copies, remote signals or barrier semaphores. Data moves between devices by JAX's collectives and lax.ppermute only.
A program may use at most 128 MiB of HBM per device.

v0:
```python
import jax
import jax.numpy as jnp
from jax import lax
from jax.sharding import Mesh, PartitionSpec as P

ADAPTER_SCALE = 2.0
EXPERT_AXES = ("zh", "y", "c")
DP_AXES = ("zl", "x")
PLANE = ("zh", "y", "c", "zl")


def dot(a, b, dims=((1,), (0,))):
    return lax.dot_general(a, b, (dims, ((), ())), preferred_element_type=jnp.float32)


def silu_slope(gate_preactivation):
    squash = jax.nn.sigmoid(gate_preactivation)
    return squash * (1.0 + gate_preactivation * (1.0 - squash))


def slot_targets(route, cap):
    rows, top = route.shape
    flat = route.T.reshape(rows * top)
    before = jnp.arange(rows * top)[:, None] > jnp.arange(rows * top)[None, :]
    same = flat[:, None] == flat[None, :]
    ranks = jnp.sum((same & before).astype(jnp.int32), axis=1)
    return (flat * cap + ranks).reshape(top, rows)


def send_places(experts, cap, swap):
    p = jnp.arange(experts * 24, dtype=jnp.int32)
    e, piece, r = (p // 24, p % 24 // 8, p % 8)
    rank = jnp.where(piece < 2, r, 8 + r % 4)
    half = jnp.where(piece < 2, piece, r // 4)
    if swap:
        half = jnp.where(e % 2 == 1, 1 - half, half)
    return (e * cap + rank, half)


def local(tokens, route, gate_output_gradient, frozen_gate_weight, adapter_first, adapter_second):
    tok_rows, width = tokens.shape
    hidden = gate_output_gradient.shape[2]
    experts = 64
    cap = 12
    zl = lax.axis_index("zl")
    mine = lax.dynamic_index_in_dim(frozen_gate_weight, zl, 0, keepdims=False)
    other = lax.dynamic_index_in_dim(frozen_gate_weight, 1 - zl, 0, keepdims=False)
    weight_near = lax.all_gather(mine, "x", axis=0, tiled=True)
    got = lax.ppermute(other, "zl", [(0, 1), (1, 0)])
    weight_far = lax.all_gather(got, "x", axis=0, tiled=True)
    first = lax.dynamic_index_in_dim(adapter_first, zl, 0, keepdims=False)
    second = lax.dynamic_index_in_dim(adapter_second, zl, 0, keepdims=False)
    half_width = width // 2
    first = jnp.where(zl == 0, first, jnp.roll(first, half_width, axis=0))
    target = slot_targets(route, cap)
    place, half = send_places(experts, cap, True)
    match = (place[:, None] == target[0][None, :]) | (place[:, None] == target[1][None, :])
    pick = jnp.concatenate([match & (half == 0)[:, None], match & (half == 1)[:, None]], axis=1)
    stack = jnp.concatenate([tokens[:, :half_width], tokens[:, half_width:]], axis=0)
    send_x = dot(pick.astype(jnp.bfloat16), stack).astype(jnp.bfloat16)
    send_x = send_x.reshape(experts, 24, half_width)
    recv_x = lax.all_to_all(send_x, PLANE, split_axis=0, concat_axis=0, tiled=True)
    place, half = send_places(experts, cap, False)
    match = place[:, None] == target.reshape(1, 2 * tok_rows)
    pick = jnp.concatenate([match & (half == 0)[:, None], match & (half == 1)[:, None]], axis=1)
    half_hidden = hidden // 2
    parts = [
        gate_output_gradient[:, k, h * half_hidden : (h + 1) * half_hidden]
        for h in range(2)
        for k in range(2)
    ]
    send_g = dot(pick.astype(jnp.bfloat16), jnp.concatenate(parts, axis=0)).astype(jnp.bfloat16)
    send_g = send_g.reshape(experts, 24, half_hidden)
    recv_g = lax.all_to_all(send_g, PLANE, split_axis=0, concat_axis=0, tiled=True)
    row = jnp.arange(4 * experts)
    col = jnp.arange(8 * experts)
    same_source = (row // 4)[:, None] == (col // 8)[None, :]

    def gather_half(received, h):
        main = received[:, 8 * h : 8 * h + 8].reshape(8 * experts, -1)
        tail = received[:, 16:24].reshape(8 * experts, -1)
        pick = same_source & ((4 * h + row % 4)[:, None] == (col % 8)[None, :])
        tail = dot(pick.astype(jnp.bfloat16), tail).astype(jnp.bfloat16)
        return jnp.concatenate([main, tail], axis=0)

    x_near = gather_half(recv_x, 0)
    x_far = gather_half(recv_x, 1)
    low = (dot(x_near, first[:half_width]) + dot(x_far, first[half_width:])).astype(jnp.bfloat16)
    frozen = dot(x_near, weight_near) + dot(x_far, weight_far)
    preact = frozen + ADAPTER_SCALE * dot(low, second)
    rows_g = jnp.concatenate([gather_half(recv_g, 0), gather_half(recv_g, 1)], axis=1)
    slope = (rows_g.astype(jnp.float32) * silu_slope(preact)).astype(jnp.bfloat16)
    back = dot(slope, second, ((1,), (1,))).astype(jnp.bfloat16)
    grads = ADAPTER_SCALE * jnp.concatenate(
        [
            dot(back, x_near, ((0,), (0,))),
            dot(back, x_far, ((0,), (0,))),
            dot(low, slope, ((0,), (0,))),
        ],
        axis=1,
    )
    rank = grads.shape[0]
    chunk = grads.shape[1] // 4
    parts = grads.reshape(rank, 4, chunk).transpose(1, 0, 2)
    parts = lax.all_to_all(parts, "x", split_axis=0, concat_axis=0, tiled=True)
    total = jnp.sum(parts, axis=0).astype(jnp.bfloat16)
    total = jnp.broadcast_to(total[None], (8, rank, chunk))
    total = lax.all_to_all(total, DP_AXES, split_axis=0, concat_axis=0, tiled=True)
    total = total.reshape(2, 4, rank, chunk).transpose(0, 2, 1, 3).reshape(2, rank, 4 * chunk)
    near, far = (total[:, :, :half_width], total[:, :, half_width:width])
    grad_a = jnp.stack(
        [jnp.concatenate([near[0], far[0]], axis=1), jnp.concatenate([far[1], near[1]], axis=1)]
    )
    grad_a = grad_a.transpose(0, 2, 1).astype(jnp.float32)
    return (grad_a, total[:, :, width:].astype(jnp.float32))


def solution(mesh):
    fine = Mesh(mesh.devices.reshape(4, 4, 2, 2, 4), EXPERT_AXES + DP_AXES)
    everyone = EXPERT_AXES + DP_AXES
    return jax.shard_map(
        local,
        mesh=fine,
        in_specs=(
            P(everyone, None),
            P(everyone, None),
            P(everyone, None, None),
            P(EXPERT_AXES, DP_AXES, None),
            P(EXPERT_AXES, None, None),
            P(EXPERT_AXES, None, None),
        ),
        out_specs=(P(EXPERT_AXES, None, None), P(EXPERT_AXES, None, None)),
        check_vma=False,
    )
```

profile of v0, /device:TPU:8, one launch (start us, length us, event | category | flops | bytes accessed | tf_op | source)
XLA Modules:
  0.0 375.5 jit_solution(1847218579089179131)
XLA Ops:
  7.2 0.9 convert_reduce_fusion
  8.9 2.8 fusion.96
  11.7 1.4 compare_and_fusion.1
  13.2 2.9 convolution_convert_fusion.1
  16.0 12.1 %all-to-all-start = ((bf16[64,24,768]{2,1,0:T(8,128)(2,1)}), bf16[64,24,768]{2,1,0:T(8,128)(2,1)S(1)}, u32[]{:S(2)}, u32[]{:S(2)}) async-start(bf16[64,24,768]{2,1,0:T(8,128)(2,1)} %bitcast.80), calls=%async_computation | async-start | bytes 4718592 | tf_op jit(solution)/shard_map/all_to_all | solution.py:74
  28.2 3.9 %dynamic-slice_bitcast_fusion = (bf16[512,1536]{1,0:T(8,128)(2,1)}, bf16[1,512,1536]{2,1,0:T(8,128)(2,1)}) fusion(bf16[2,512,1536]{2,1,0:T(8,128)(2,1)} %param.9, s32[]{:T(128)S(6)} %select_n.335, s32[]{:T(128)S(6)} %select_n.334), kind=kLoop, calls=%fused_computation.17 | loop fusion | bytes 6291464 | tf_op jit(solution)/shard_map/jit(dynamic_index_in_dim)/squeeze | solution.py:47
  32.2 1.4 fusion.23
  33.7 4.5 %convolution_convert_fusion = bf16[1536,2048]{1,0:T(8,128)(2,1)} fusion(pred[1536,128]{1,0:T(32,128)(4,1)S(1)} %get-tuple-element.23, pred[1536,128]{1,0:T(32,128)(4,1)S(1)} %get-tuple-element.22, bf16[128,2048]{1,0:T(8,128)(2,1)S(1)} %get-tuple-element.9, bf16[128,2048]{1,0:T(8,128)(2,1)S(1)} %get-tuple-element.8), kind=kOutput, calls=%fused_computation | convolution fusion | flops 1616248832 | bytes 7733248 | tf_op jit(solution)/shard_map/dot_general | solution.py:13
  38.1 46.8 %all-to-all-done = bf16[64,24,768]{2,1,0:T(8,128)(2,1)S(1)} async-done(((bf16[64,24,768]{2,1,0:T(8,128)(2,1)}), bf16[64,24,768]{2,1,0:T(8,128)(2,1)S(1)}, u32[]{:S(2)}, u32[]{:S(2)}) %all-to-all-start) | async-done | bytes 2359328 | tf_op jit(solution)/shard_map/all_to_all | solution.py:74
  84.9 5.8 %all-to-all-start.1 = ((bf16[64,24,2048]{2,1,0:T(8,128)(2,1)}), bf16[64,24,2048]{2,1,0:T(8,128)(2,1)}, u32[]{:S(2)}, u32[]{:S(2)}) async-start(bf16[64,24,2048]{2,1,0:T(8,128)(2,1)} %bitcast.79), calls=%async_computation.1 | async-start | bytes 12582912 | tf_op jit(solution)/shard_map/all_to_all | solution.py:62
  90.8 1.7 collective-permute-start
  92.5 169.0 %collective-permute-done = bf16[512,1536]{1,0:T(8,128)(2,1)} collective-permute-done((bf16[512,1536]{1,0:T(8,128)(2,1)}, bf16[512,1536]{1,0:T(8,128)(2,1)}, u32[]{:S(2)}, u32[]{:S(2)}) %collective-permute-start) | collective-permute-done | bytes 1572896 | tf_op jit(solution)/shard_map/ppermute | solution.py:49
  261.6 1.2 convolution_convert_fusion.5
  262.8 1.2 convolution_convert_fusion.4
  264.0 1.1 slice_bitcast_fusion.7
  265.1 2.4 convolution_convert_fusion.3
  267.4 3.0 slice_bitcast_fusion
  271.4 2.4 convolution_convert_fusion.2
  274.8 2.9 fusion.44
  277.7 9.7 %fusion = f32[768,1536]{1,0:T(8,128)} fusion(bf16[1,2048,1536]{2,1,0:T(8,128)(2,1)} %all-gather.6.cloned.1.call-done, bf16[256,2048]{1,0:T(8,128)(2,1)} %copy-done.5, bf16[512,2048]{1,0:T(8,128)(2,1)} %copy-done.1), kind=kOutput, calls=%fused_computation.1 | convolution fusion | flops 4838129664 | bytes 14155776 | tf_op jit(solution)/shard_map/dot_general | solution.py:13
  287.4 42.7 %all-gather.4.cloned.1.call-done = bf16[2048,1536]{1,0:T(8,128)(2,1)} async-done(((bf16[512,1536]{1,0:T(8,128)(2,1)}), bf16[2048,1536]{1,0:T(8,128)(2,1)}) %all-gather.4.cloned.1.call-update) | async-done | bytes 6291472 | tf_op jit(solution)/shard_map/all_gather | solution.py:50
  330.1 12.5 %multiply_convert_fusion = bf16[768,1536]{1,0:T(8,128)(2,1)S(1)} fusion(f32[768,1536]{1,0:T(8,128)} %fusion.44, f32[768,1536]{1,0:T(8,128)} %fusion, bf16[2048,1536]{1,0:T(8,128)(2,1)} %all-gather.4.cloned.1.call-done, bf16[256,768]{1,0:T(8,128)(2,1)} %convolution_convert_fusion.4, bf16[512,768]{1,0:T(8,128)(2,1)} %get-tuple-element.7, ...), kind=kOutput, calls=%fused_computation.3 | convolution fusion | flops 4861722624 | bytes 23592960 | tf_op jit(solution)/shard_map/dot_general | solution.py:13
  344.9 11.0 %all_to_all.20 = f32[4,16,1408]{2,1,0:T(8,128)S(1)} all-to-all(f32[4,16,1408]{2,1,0:T(8,128)S(1)} %bitcast.84), channel_id=1, replica_groups=mesh['zh'=4,'y'=4,'c'=2,'zl'=2,'x'=4] {'x'}, dimensions={0} | all-to-all | bytes 720896 | tf_op jit(solution)/shard_map/all_to_all | solution.py:105
  356.0 11.1 %all_to_all.21 = bf16[8,16,1408]{2,1,0:T(8,128)(2,1)S(1)} all-to-all(bf16[8,16,1408]{2,1,0:T(8,128)(2,1)S(1)} %broadcast_in_dim.2), channel_id=1, replica_groups=mesh['zh'=4,'y'=4,'c'=2,'zl'=2,'x'=4] {'zl','x'}, dimensions={0} | all-to-all | bytes 720896 | tf_op jit(solution)/shard_map/all_to_all | solution.py:108
  (53 shorter events, 7.0 us)
Async XLA Ops:
  7.2 267.6 %copy-start = (bf16[2,16,1536]{2,1,0:T(8,128)(2,1)S(1)}, bf16[2,16,1536]{2,1,0:T(8,128)(2,1)}, u32[]{:S(2)}) copy-start(bf16[2,16,1536]{2,1,0:T(8,128)(2,1)} %param.11) | copy-start | bytes 294916
  16.0 68.9 %all-to-all-start = ((bf16[64,24,768]{2,1,0:T(8,128)(2,1)}), bf16[64,24,768]{2,1,0:T(8,128)(2,1)S(1)}, u32[]{:S(2)}, u32[]{:S(2)}) async-start(bf16[64,24,768]{2,1,0:T(8,128)(2,1)} %bitcast.80), calls=%async_computation | async-start | bytes 4718592 | tf_op jit(solution)/shard_map/all_to_all | solution.py:74
  28.1 249.5 %all-gather.6.cloned.1.call-start = ((), (), s32[]{:S(2)}) async-start(), calls=%async_computation.5 | async-start | bytes 7864320 | tf_op jit(solution)/shard_map/all_gather | solution.py:48
  28.2 5.4 %copy-start.3 = (bf16[128,4096]{1,0:T(8,128)(2,1)S(1)}, bf16[128,4096]{1,0:T(8,128)(2,1)}, u32[]{:S(2)}) copy-start(bf16[128,4096]{1,0:T(8,128)(2,1)} %param.6) | copy-start | bytes 3145732
  84.9 176.7 %copy-start.4 = (bf16[2,4096,16]{1,2,0:T(8,128)(2,1)S(1)}, bf16[2,4096,16]{1,2,0:T(8,128)(2,1)}, u32[]{:S(2)}) copy-start(bf16[2,4096,16]{1,2,0:T(8,128)(2,1)} %param.10) | copy-start | bytes 786436
  84.9 180.2 %all-to-all-start.1 = ((bf16[64,24,2048]{2,1,0:T(8,128)(2,1)}), bf16[64,24,2048]{2,1,0:T(8,128)(2,1)}, u32[]{:S(2)}, u32[]{:S(2)}) async-start(bf16[64,24,2048]{2,1,0:T(8,128)(2,1)} %bitcast.79), calls=%async_computation.1 | async-start | bytes 12582912 | tf_op jit(solution)/shard_map/all_to_all | solution.py:62
  90.7 239.4 %all-gather.4.cloned.1.call-start = ((), (), s32[]{:S(2)}) async-start(), calls=%async_computation.4 | async-start | bytes 7864320 | tf_op jit(solution)/shard_map/all_gather | solution.py:50
  90.8 170.7 %collective-permute-start = (bf16[512,1536]{1,0:T(8,128)(2,1)}, bf16[512,1536]{1,0:T(8,128)(2,1)}, u32[]{:S(2)}, u32[]{:S(2)}) collective-permute-start(bf16[512,1536]{1,0:T(8,128)(2,1)} %get-tuple-element.4), channel_id=1, source_target_pairs={{0,4},{4,0},{1,5},{5,1},{2,6},{6,2},{3,7},{7,3},{8,12},{12,8},{9,1... | collective-permute-start | bytes 4718600 | tf_op jit(solution)/shard_map/ppermute | solution.py:49
  267.4 3.0 copy-start.5
  270.4 3.3 copy-start.1
  273.8 1.0 copy-start.7
  330.1 13.2 %copy-start.2 = (bf16[512,2048]{1,0:T(8,128)(2,1)S(1)}, bf16[512,2048]{1,0:T(8,128)(2,1)}, u32[]{:S(2)}) copy-start(bf16[512,2048]{1,0:T(8,128)(2,1)} %copy-done.1) | copy-start | bytes 6291460
  330.1 13.2 %copy-start.6 = (bf16[256,2048]{1,0:T(8,128)(2,1)S(1)}, bf16[256,2048]{1,0:T(8,128)(2,1)}, u32[]{:S(2)}) copy-start(bf16[256,2048]{1,0:T(8,128)(2,1)} %copy-done.5) | copy-start | bytes 3145732
  342.6 1.3 copy-start.8
Sparse Core Ops, SparseCore 0:
  32.3 69.2 all-gather.5
  261.6 68.4 all-gather.3
where the time goes:
time: 376 us
  waiting for transfers between devices  259 us (69%)
  matrix products  43.6 us (12%)
  blocking collectives  22.1 us (6%)
  starting transfers between devices  19.7 us (5%)
  between operations  14.3 us (4%)
  local copies, waits for them, and re-layouts  11.2 us (3%)
  other arithmetic  6.15 us (2%)
    ppermute x1, waiting for transfers between devices, local(): got = lax.ppermute(other, 'zl', [(0, 1), (1, 0)])  169 us
    all_to_all x1, waiting for transfers between devices, local(): lax.all_to_all(send_g, PLANE, split_axis=0, concat_axis=0, tiled=True)  46.8 us
    dot_general x15, matrix products, dot(): lax.dot_general(a, b, (dims, ((), ())), preferred_element_type=jnp.float32)  43.6 us
    all_gather x1, waiting for transfers between devices, local(): weight_far = lax.all_gather(got, 'x', axis=0, tiled=True)  42.7 us
    all_to_all x1, starting transfers between devices, local(): lax.all_to_all(send_g, PLANE, split_axis=0, concat_axis=0, tiled=True)  12.1 us
    all_to_all x1, blocking collectives, local(): lax.all_to_all(total, DP_AXES, split_axis=0, concat_axis=0, tiled=True)  11.1 us
    all_to_all x1, blocking collectives, local(): parts = lax.all_to_all(parts, 'x', split_axis=0, concat_axis=0, tiled=True)  11 us
  transfers between devices with their start and end apart: 5, of which 3 were waited for; matrix products, arithmetic and copies ran while one was open for 9% of the time, Pallas kernels for 0%

commit v1 on v0

--- a/solution.py
+++ b/solution.py
@@ -47,7 +47,9 @@
     other = lax.dynamic_index_in_dim(frozen_gate_weight, 1 - zl, 0, keepdims=False)
     weight_near = lax.all_gather(mine, "x", axis=0, tiled=True)
     got = lax.ppermute(other, "zl", [(0, 1), (1, 0)])
-    weight_far = lax.all_gather(got, "x", axis=0, tiled=True)
+    weight_far = jnp.concatenate(
+        lax.all_to_all(jnp.stack([got] * lax.axis_size("x")), "x", 0, 0), axis=0
+    )
     first = lax.dynamic_index_in_dim(adapter_first, zl, 0, keepdims=False)
     second = lax.dynamic_index_in_dim(adapter_second, zl, 0, keepdims=False)
     half_width = width // 2

time: 376 us -> 387 us (1.029)
  starting transfers between devices: 19.7 us -> 25 us
  local copies, waits for them, and re-layouts: 11.2 us -> 15.4 us
    all_to_all x0 -> x1, waiting for transfers between devices: none -> 46.1 us  [local(): lax.all_to_all(jnp.stack([got] * lax.axis_size('x')), 'x', 0, 0)]
    all_gather x1 -> x0, waiting for transfers between devices: 42.7 us -> none  [local(): weight_far = lax.all_gather(got, 'x', axis=0, tiled=True)]
    all_to_all x0 -> x1, starting transfers between devices: none -> 5.54 us  [local(): lax.all_to_all(jnp.stack([got] * lax.axis_size('x')), 'x', 0, 0)]
    another operation x0 -> x1, local copies, waits for them, and re-layouts: none -> 4.48 us  [local(): jnp.stack([got] * lax.axis_size('x'))]
    all_to_all x1, waiting for transfers between devices: 46.8 us -> 50.8 us  [local(): lax.all_to_all(send_g, PLANE, split_axis=0, concat_axis=0, tiled=True)]
  transfers between devices with their start and end apart: 5 -> 5, of which waited for: 3 -> 3; matrix products, arithmetic and copies ran while one was open for 9% -> 10% of each run, Pallas kernels for 0% -> 0%
where the time goes in v1:
time: 387 us; the launch traced here: 386 us
  waiting for transfers between devices  262 us (68%)
  matrix products  43 us (11%)
  starting transfers between devices  25 us (6%)
  blocking collectives  19.8 us (5%)
  local copies, waits for them, and re-layouts  15.4 us (4%)
  between operations  14.3 us (4%)
  other arithmetic  6.15 us (2%)
    ppermute x1, waiting for transfers between devices, local(): got = lax.ppermute(other, 'zl', [(0, 1), (1, 0)])  165 us
    all_to_all x1, waiting for transfers between devices, local(): lax.all_to_all(send_g, PLANE, split_axis=0, concat_axis=0, tiled=True)  50.8 us
    all_to_all x1, waiting for transfers between devices, local(): lax.all_to_all(jnp.stack([got] * lax.axis_size('x')), 'x', 0, 0)  46.1 us
    dot_general x15, matrix products, dot(): lax.dot_general(a, b, (dims, ((), ())), preferred_element_type=jnp.float32)  43 us
    all_to_all x1, starting transfers between devices, local(): lax.all_to_all(send_g, PLANE, split_axis=0, concat_axis=0, tiled=True)  12.2 us
    all_to_all x1, blocking collectives, local(): lax.all_to_all(total, DP_AXES, split_axis=0, concat_axis=0, tiled=True)  10.2 us
    all_to_all x1, blocking collectives, local(): parts = lax.all_to_all(parts, 'x', split_axis=0, concat_axis=0, tiled=True)  9.59 us
  transfers between devices with their start and end apart: 5, of which 3 were waited for; matrix products, arithmetic and copies ran while one was open for 10% of the time, Pallas kernels for 0%

profile of v1, /device:TPU:8, one launch (start us, length us, event | category | flops | bytes accessed | tf_op | source)
XLA Modules:
  0.0 386.0 jit_solution(11924985710725054050)
XLA Ops:
  8.9 2.7 fusion.96
  11.7 1.4 compare_and_fusion.1
  13.1 2.8 convolution_convert_fusion.1
  15.9 12.2 %all-to-all-start = ((bf16[64,24,768]{2,1,0:T(8,128)(2,1)}), bf16[64,24,768]{2,1,0:T(8,128)(2,1)S(1)}, u32[]{:S(2)}, u32[]{:S(2)}) async-start(bf16[64,24,768]{2,1,0:T(8,128)(2,1)} %bitcast.81), calls=%async_computation | async-start | bytes 4718592 | tf_op jit(solution)/shard_map/all_to_all | solution.py:76
  28.2 1.4 fusion.23
  29.7 4.4 %convolution_convert_fusion = bf16[1536,2048]{1,0:T(8,128)(2,1)} fusion(pred[1536,128]{1,0:T(32,128)(4,1)S(1)} %get-tuple-element.23, pred[1536,128]{1,0:T(32,128)(4,1)S(1)} %get-tuple-element.22, bf16[128,2048]{1,0:T(8,128)(2,1)S(1)} %get-tuple-element.9, bf16[128,2048]{1,0:T(8,128)(2,1)S(1)} %get-tuple-element.8), kind=kOutput, calls=%fused_computation | convolution fusion | flops 1616248832 | bytes 7733248 | tf_op jit(solution)/shard_map/dot_general | solution.py:13
  34.1 50.8 %all-to-all-done = bf16[64,24,768]{2,1,0:T(8,128)(2,1)S(1)} async-done(((bf16[64,24,768]{2,1,0:T(8,128)(2,1)}), bf16[64,24,768]{2,1,0:T(8,128)(2,1)S(1)}, u32[]{:S(2)}, u32[]{:S(2)}) %all-to-all-start) | async-done | bytes 2359328 | tf_op jit(solution)/shard_map/all_to_all | solution.py:76
  84.9 5.7 %all-to-all-start.1 = ((bf16[64,24,2048]{2,1,0:T(8,128)(2,1)}), bf16[64,24,2048]{2,1,0:T(8,128)(2,1)}, u32[]{:S(2)}, u32[]{:S(2)}) async-start(bf16[64,24,2048]{2,1,0:T(8,128)(2,1)} %bitcast.80), calls=%async_computation.1 | async-start | bytes 12582912 | tf_op jit(solution)/shard_map/all_to_all | solution.py:64
  90.7 3.8 dynamic-slice_bitcast_fusion
  94.5 1.6 collective-permute-start
  96.1 165.3 %collective-permute-done = bf16[512,1536]{1,0:T(8,128)(2,1)} collective-permute-done((bf16[512,1536]{1,0:T(8,128)(2,1)}, bf16[512,1536]{1,0:T(8,128)(2,1)}, u32[]{:S(2)}, u32[]{:S(2)}) %collective-permute-start) | collective-permute-done | bytes 1572896 | tf_op jit(solution)/shard_map/ppermute | solution.py:49
  261.4 4.5 %stack.16 = bf16[4,512,1536]{2,1,0:T(8,128)(2,1)} broadcast(bf16[512,1536]{1,0:T(8,128)(2,1)} %collective-permute-done), dimensions={1,2} | broadcast | bytes 7864320 | tf_op jit(solution)/shard_map/stack | solution.py:51
  265.9 5.5 %all-to-all-start.2 = ((bf16[4,512,1536]{2,1,0:T(8,128)(2,1)}), bf16[4,512,1536]{2,1,0:T(8,128)(2,1)}, u32[]{:S(2)}, u32[]{:S(2)}) async-start(bf16[4,512,1536]{2,1,0:T(8,128)(2,1)} %stack.16), calls=%async_computation.2 | async-start | bytes 12582912 | tf_op jit(solution)/shard_map/all_to_all | solution.py:51
  271.5 1.2 convolution_convert_fusion.4
  272.7 1.2 convolution_convert_fusion.5
  274.9 2.4 convolution_convert_fusion.3
  277.3 3.0 slice_bitcast_fusion
  281.2 2.4 convolution_convert_fusion.2
  284.6 3.0 fusion.44
  287.6 8.9 %fusion = f32[768,1536]{1,0:T(8,128)} fusion(bf16[1,2048,1536]{2,1,0:T(8,128)(2,1)} %all-gather.3.cloned.1.call-done, bf16[256,2048]{1,0:T(8,128)(2,1)} %copy-done.5, bf16[512,2048]{1,0:T(8,128)(2,1)S(1)} %get-tuple-element.3), kind=kOutput, calls=%fused_computation.1 | convolution fusion | flops 4838129664 | bytes 14155776 | tf_op jit(solution)/shard_map/dot_general | solution.py:13
  296.5 46.1 %all-to-all-done.2 = bf16[4,512,1536]{2,1,0:T(8,128)(2,1)} async-done(((bf16[4,512,1536]{2,1,0:T(8,128)(2,1)}), bf16[4,512,1536]{2,1,0:T(8,128)(2,1)}, u32[]{:S(2)}, u32[]{:S(2)}) %all-to-all-start.2) | async-done | bytes 6291488 | tf_op jit(solution)/shard_map/all_to_all | solution.py:51
  342.6 12.8 %multiply_convert_fusion = bf16[768,1536]{1,0:T(8,128)(2,1)S(1)} fusion(f32[768,1536]{1,0:T(8,128)} %fusion.44, f32[768,1536]{1,0:T(8,128)} %fusion, bf16[2048,1536]{1,0:T(8,128)(2,1)} %bitcast.17, bf16[256,768]{1,0:T(8,128)(2,1)} %convolution_convert_fusion.4, bf16[512,768]{1,0:T(8,128)(2,1)} %get-tuple-element.7, ...), kind=kOutput, calls=%fused_computation.3 | convolution fusion | flops 4861722624 | bytes 23592960 | tf_op jit(solution)/shard_map/dot_general | solution.py:13
  357.6 9.6 %all_to_all.25 = f32[4,16,1408]{2,1,0:T(8,128)S(1)} all-to-all(f32[4,16,1408]{2,1,0:T(8,128)S(1)} %bitcast.85), channel_id=1, replica_groups=mesh['zh'=4,'y'=4,'c'=2,'zl'=2,'x'=4] {'x'}, dimensions={0} | all-to-all | bytes 720896 | tf_op jit(solution)/shard_map/all_to_all | solution.py:107
  367.3 10.2 %all_to_all.26 = bf16[8,16,1408]{2,1,0:T(8,128)(2,1)S(1)} all-to-all(bf16[8,16,1408]{2,1,0:T(8,128)(2,1)S(1)} %broadcast_in_dim.2), channel_id=1, replica_groups=mesh['zh'=4,'y'=4,'c'=2,'zl'=2,'x'=4] {'zl','x'}, dimensions={0} | all-to-all | bytes 720896 | tf_op jit(solution)/shard_map/all_to_all | solution.py:110
  (53 shorter events, 8.8 us)
Async XLA Ops:
  7.2 277.4 %copy-start = (bf16[2,16,1536]{2,1,0:T(8,128)(2,1)S(1)}, bf16[2,16,1536]{2,1,0:T(8,128)(2,1)}, u32[]{:S(2)}) copy-start(bf16[2,16,1536]{2,1,0:T(8,128)(2,1)} %param.11) | copy-start | bytes 294916
  15.9 13.7 %copy-start.3 = (bf16[128,4096]{1,0:T(8,128)(2,1)S(1)}, bf16[128,4096]{1,0:T(8,128)(2,1)}, u32[]{:S(2)}) copy-start(bf16[128,4096]{1,0:T(8,128)(2,1)} %param.6) | copy-start | bytes 3145732
  15.9 69.0 %all-to-all-start = ((bf16[64,24,768]{2,1,0:T(8,128)(2,1)}), bf16[64,24,768]{2,1,0:T(8,128)(2,1)S(1)}, u32[]{:S(2)}, u32[]{:S(2)}) async-start(bf16[64,24,768]{2,1,0:T(8,128)(2,1)} %bitcast.81), calls=%async_computation | async-start | bytes 4718592 | tf_op jit(solution)/shard_map/all_to_all | solution.py:76
  84.9 176.5 %all-to-all-start.1 = ((bf16[64,24,2048]{2,1,0:T(8,128)(2,1)}), bf16[64,24,2048]{2,1,0:T(8,128)(2,1)}, u32[]{:S(2)}, u32[]{:S(2)}) async-start(bf16[64,24,2048]{2,1,0:T(8,128)(2,1)} %bitcast.80), calls=%async_computation.1 | async-start | bytes 12582912 | tf_op jit(solution)/shard_map/all_to_all | solution.py:64
  90.6 197.0 %all-gather.3.cloned.1.call-start = ((), (), s32[]{:S(2)}) async-start(), calls=%async_computation.5 | async-start | bytes 7864320 | tf_op jit(solution)/shard_map/all_gather | solution.py:48
  94.5 166.9 %collective-permute-start = (bf16[512,1536]{1,0:T(8,128)(2,1)}, bf16[512,1536]{1,0:T(8,128)(2,1)}, u32[]{:S(2)}, u32[]{:S(2)}) collective-permute-start(bf16[512,1536]{1,0:T(8,128)(2,1)} %get-tuple-element.4), channel_id=1, source_target_pairs={{0,4},{4,0},{1,5},{5,1},{2,6},{6,2},{3,7},{7,3},{8,12},{12,8},{9,1... | collective-permute-start | bytes 4718600 | tf_op jit(solution)/shard_map/ppermute | solution.py:49
  265.9 5.6 %copy-start.4 = (bf16[2,4096,16]{1,2,0:T(8,128)(2,1)S(1)}, bf16[2,4096,16]{1,2,0:T(8,128)(2,1)}, u32[]{:S(2)}) copy-start(bf16[2,4096,16]{1,2,0:T(8,128)(2,1)} %param.10) | copy-start | bytes 786436
  265.9 76.7 %all-to-all-start.2 = ((bf16[4,512,1536]{2,1,0:T(8,128)(2,1)}), bf16[4,512,1536]{2,1,0:T(8,128)(2,1)}, u32[]{:S(2)}, u32[]{:S(2)}) async-start(bf16[4,512,1536]{2,1,0:T(8,128)(2,1)} %stack.16), calls=%async_computation.2 | async-start | bytes 12582912 | tf_op jit(solution)/shard_map/all_to_all | solution.py:51
  277.3 3.0 copy-start.5
  280.3 3.3 copy-start.1
  283.6 1.0 copy-start.7
  342.6 13.5 %copy-start.2 = (bf16[512,2048]{1,0:T(8,128)(2,1)S(1)}, bf16[512,2048]{1,0:T(8,128)(2,1)}, u32[]{:S(2)}) copy-start(bf16[512,2048]{1,0:T(8,128)(2,1)} %copy-done.1) | copy-start | bytes 6291460
  342.6 13.5 %copy-start.8 = (bf16[256,2048]{1,0:T(8,128)(2,1)S(1)}, bf16[256,2048]{1,0:T(8,128)(2,1)}, u32[]{:S(2)}) copy-start(bf16[256,2048]{1,0:T(8,128)(2,1)} %copy-done.7) | copy-start | bytes 3145732
  355.3 1.3 copy-start.6
Sparse Core Ops, SparseCore 0:
  94.7 69.2 all-gather.2
